TPU v7x, 32 devices: a whole 2x2x4 slice. The times are simulated.
32 devices in a mesh: fsdp: 2 (over x), ctx: 4 (over z), tp: 4 (over y, core).
Axes of the slice: x: 2, y: 2, z: 4, core: 2. Of those that a mesh axis runs over, the one named last changes fastest.
Arguments:
- tokens: bfloat16 [2, 1024, 2048], P('fsdp', 'ctx'), may hold values from -6 to 6
- log_decay: float32 [2, 1024, 8], P('fsdp', 'ctx', 'tp'), may hold values from -0.6 to 0, as said below
- w_query: bfloat16 [2048, 2048], P(('fsdp', 'ctx'), 'tp'), may hold values from -0.125 to 0.125
- w_key: bfloat16 [2048, 2048], P(('fsdp', 'ctx'), 'tp'), may hold values from -0.125 to 0.125
- w_value: bfloat16 [2048, 4096], P(('fsdp', 'ctx'), 'tp'), may hold values from -0.125 to 0.125
- w_gate: bfloat16 [2048, 4096], P(('fsdp', 'ctx'), 'tp'), may hold values from -0.125 to 0.125
- w_out: bfloat16 [2048, 4096], P(('fsdp', 'ctx'), 'tp'), may hold values from -0.125 to 0.125
- norm1_gain: bfloat16 [2048], P(('fsdp', 'ctx')), may hold values from 0.099609375 to 1.8984375
- norm1_bias: bfloat16 [2048], P(('fsdp', 'ctx')), may hold values from -3 to 3
- w_ffgate: bfloat16 [2048, 4096], P(('fsdp', 'ctx'), 'tp'), may hold values from -0.125 to 0.125
- w_ffup: bfloat16 [2048, 4096], P(('fsdp', 'ctx'), 'tp'), may hold values from -0.125 to 0.125
- w_down: bfloat16 [2048, 4096], P(('fsdp', 'ctx'), 'tp'), may hold values from -0.125 to 0.125
- norm2_gain: bfloat16 [2048], P(('fsdp', 'ctx')), may hold values from 0.099609375 to 1.8984375
- norm2_bias: bfloat16 [2048], P(('fsdp', 'ctx')), may hold values from -3 to 3
- grad_out: bfloat16 [2, 1024, 2048], P('fsdp', 'ctx'), may hold values from -6 to 6
Outputs:
- output: bfloat16 [2, 1024, 2048], P('fsdp', 'ctx')
- grad_tokens: bfloat16 [2, 1024, 2048], P('fsdp', 'ctx')
- grad_w_query: float32 [2048, 2048], P(('fsdp', 'ctx'), 'tp')
- grad_w_key: float32 [2048, 2048], P(('fsdp', 'ctx'), 'tp')
- grad_w_value: float32 [2048, 4096], P(('fsdp', 'ctx'), 'tp')
- grad_w_gate: float32 [2048, 4096], P(('fsdp', 'ctx'), 'tp')
- grad_w_out: float32 [2048, 4096], P(('fsdp', 'ctx'), 'tp')
- grad_norm1_gain: float32 [2048], P(('fsdp', 'ctx'))
- grad_norm1_bias: float32 [2048], P(('fsdp', 'ctx'))
- grad_w_ffgate: float32 [2048, 4096], P(('fsdp', 'ctx'), 'tp')
- grad_w_ffup: float32 [2048, 4096], P(('fsdp', 'ctx'), 'tp')
- grad_w_down: float32 [2048, 4096], P(('fsdp', 'ctx'), 'tp')
- grad_norm2_gain: float32 [2048], P(('fsdp', 'ctx'))
- grad_norm2_bias: float32 [2048], P(('fsdp', 'ctx'))
Inputs may be any that keep to these rules, and one draw needn't show every extreme that they name: `log_decay`: log of the factor by which a head's state shrinks at a position.
All inputs are finite; a program needn't handle non-finite values.
Results may differ from a plain program's by a relative error of at most 0.018.
Values may be sent and summed in bfloat16 or wider, within the bound.
A program may use at most 192 MiB of HBM per device.

v0:
```python
import jax
import jax.numpy as jnp
from jax import lax
from jax.sharding import PartitionSpec as P

KEY = 256
HEAD_V = 512


EPSILON = 1e-05
PRECISE = lax.Precision.HIGHEST
CONTRACT_LAST = (((1,), (1,)), ((), ()))
CONTRACT_FIRST = (((0,), (0,)), ((), ()))


def carried_in(part, axis, combine, identity, reverse):
    count = lax.axis_size(axis)
    place = lax.axis_index(axis)
    ahead = count - 1 - place if reverse else place
    gathered = jax.tree.map(lambda a: lax.all_gather(a, axis), part)
    state = jax.tree.map(lambda a, e: jnp.zeros_like(a) + jnp.asarray(e, a.dtype), part, identity)

    def one(step, state):
        source = count - 1 - step if reverse else step
        return combine(
            state, jax.tree.map(lambda a: lax.dynamic_index_in_dim(a, source, 0, False), gathered)
        )

    return lax.fori_loop(0, ahead, one, state)


def layer_norm(values, scaling, offset):
    center = values - jnp.mean(values, axis=-1, keepdims=True)
    spread = jnp.mean(center * center, axis=-1, keepdims=True)
    return center * lax.rsqrt(spread + EPSILON) * scaling + offset


def gate_norm(gate_vals, mixed_vals):
    center = mixed_vals - jnp.mean(mixed_vals, axis=-1, keepdims=True)
    spread = jnp.mean(center * center, axis=-1, keepdims=True)
    normal = center * lax.rsqrt(spread + EPSILON)
    return jax.nn.silu(gate_vals) * normal.reshape(gate_vals.shape)


def gelu_gate(ff_gate, ff_up):
    return jax.nn.gelu(ff_gate, approximate=True) * ff_up


def combine(earlier, latter):
    return (earlier[0] * latter[0], latter[0][:, :, None, None] * earlier[1] + latter[1])


def product(operand, other):
    return jnp.dot(operand, other, preferred_element_type=jnp.float32)


def product_last(operand, other):
    return lax.dot_general(operand, other, CONTRACT_LAST, preferred_element_type=jnp.float32)


def product_first(operand, other):
    return lax.dot_general(operand, other, CONTRACT_FIRST, preferred_element_type=jnp.float32)


def shards(
    tokens,
    log_decay,
    w_query,
    w_key,
    w_value,
    w_gate,
    w_out,
    norm1_gain,
    norm1_bias,
    w_ffgate,
    w_ffup,
    w_down,
    norm2_gain,
    norm2_bias,
    grad_out,
):
    seqs_here, block_len, width = tokens.shape
    heads_here = log_decay.shape[2]
    row_count = seqs_here * block_len
    key_shape = (seqs_here, block_len, heads_here, KEY)
    value_shape = (seqs_here, block_len, heads_here, HEAD_V)
    score_scale = float(KEY) ** (-0.5)
    mixer_weights = (
        lax.all_gather(w_query, ("fsdp", "ctx"), axis=0, tiled=True),
        lax.all_gather(w_key, ("fsdp", "ctx"), axis=0, tiled=True),
        lax.all_gather(w_value, ("fsdp", "ctx"), axis=0, tiled=True),
        lax.all_gather(w_gate, ("fsdp", "ctx"), axis=0, tiled=True),
        lax.all_gather(w_out, ("fsdp", "ctx"), axis=0, tiled=True),
        lax.all_gather(norm1_gain, ("fsdp", "ctx"), axis=0, tiled=True),
        lax.all_gather(norm1_bias, ("fsdp", "ctx"), axis=0, tiled=True),
    )
    full_query, full_key, full_value, full_gate, full_out, first_gain, first_bias = mixer_weights
    flat_tokens = tokens.astype(jnp.float32).reshape(row_count, width)
    normed_float, norm_pull = jax.vjp(
        layer_norm, flat_tokens, first_gain.astype(jnp.float32), first_bias.astype(jnp.float32)
    )
    normed = normed_float.astype(jnp.bfloat16)
    queries = product(normed, full_query).astype(jnp.bfloat16)
    key_rows = product(normed, full_key).astype(jnp.bfloat16)
    value_rows = product(normed, full_value).astype(jnp.bfloat16)
    gate_rows = product(normed, full_gate).astype(jnp.bfloat16)
    query_block = queries.reshape(key_shape)
    key_block = key_rows.reshape(key_shape)
    value_block = value_rows.reshape(value_shape)
    query_float = query_block.astype(jnp.float32)
    key_float = key_block.astype(jnp.float32)
    value_float = value_block.astype(jnp.float32)
    cumulative = jnp.cumsum(log_decay, axis=1)
    block_total = cumulative[:, -1, :]
    by_head = jnp.transpose(cumulative, (0, 2, 1))
    positions = jnp.arange(block_len)
    causal = positions[:, None] >= positions[None, :]
    decay_table = jnp.where(
        causal, jnp.exp(jnp.minimum(by_head[:, :, :, None] - by_head[:, :, None, :], 0.0)), 0.0
    )
    scores = jnp.einsum(
        "bthd,bshd->bhts", query_block, key_block, preferred_element_type=jnp.float32
    )
    weights = (scores * score_scale * decay_table).astype(jnp.bfloat16)
    growth = jnp.exp(cumulative)[:, :, :, None]
    keeping = jnp.exp(block_total[:, None, :] - cumulative)[:, :, :, None]
    fresh_state = jnp.einsum("bshd,bshe->bhde", key_float * keeping, value_float, precision=PRECISE)
    through = jnp.exp(block_total)
    no_decay = jnp.ones_like(through)
    no_state = jnp.zeros_like(fresh_state)
    carried = carried_in((through, fresh_state), "ctx", combine, (no_decay, no_state), False)
    incoming = carried[1]
    mixer_out = jnp.einsum(
        "bhts,bshe->bthe", weights, value_block, preferred_element_type=jnp.float32
    )
    mixer_out = mixer_out + jnp.einsum(
        "bthd,bhde->bthe", query_float * growth, incoming, precision=PRECISE
    )
    gated_float, gate_pull = jax.vjp(
        gate_norm, gate_rows.astype(jnp.float32), mixer_out.reshape(row_count, heads_here, HEAD_V)
    )
    gated_out = gated_float.astype(jnp.bfloat16)
    middle = flat_tokens + lax.psum(product_last(gated_out, full_out), "tp")
    mlp_weights = (
        lax.all_gather(w_ffgate, ("fsdp", "ctx"), axis=0, tiled=True),
        lax.all_gather(w_ffup, ("fsdp", "ctx"), axis=0, tiled=True),
        lax.all_gather(w_down, ("fsdp", "ctx"), axis=0, tiled=True),
        lax.all_gather(norm2_gain, ("fsdp", "ctx"), axis=0, tiled=True),
        lax.all_gather(norm2_bias, ("fsdp", "ctx"), axis=0, tiled=True),
    )
    full_gating, full_upward, full_downward, second_gain, second_bias = mlp_weights
    second_float, second_pull = jax.vjp(
        layer_norm, middle, second_gain.astype(jnp.float32), second_bias.astype(jnp.float32)
    )
    second_normed = second_float.astype(jnp.bfloat16)
    ff_gate = product(second_normed, full_gating).astype(jnp.bfloat16)
    ff_up = product(second_normed, full_upward).astype(jnp.bfloat16)
    hidden_float, gelu_pull = jax.vjp(
        gelu_gate, ff_gate.astype(jnp.float32), ff_up.astype(jnp.float32)
    )
    hidden = hidden_float.astype(jnp.bfloat16)
    down_terms = product_last(hidden, full_downward)
    result = middle + lax.psum(down_terms, "tp")
    output = result.astype(jnp.bfloat16).reshape(tokens.shape)
    upstream = grad_out.reshape(row_count, width)
    back_gating, back_upward, back_downward = (full_gating, full_upward, full_downward)
    grad_hidden = product(upstream, back_downward)
    pulled_gate, pulled_up = gelu_pull(grad_hidden)
    grad_ffgate = pulled_gate.astype(jnp.bfloat16)
    grad_ffup = pulled_up.astype(jnp.bfloat16)
    grad_second = product_last(grad_ffgate, back_gating) + product_last(grad_ffup, back_upward)
    downward_grad = product_first(upstream, hidden)
    gating_grad = product_first(second_normed, grad_ffgate)
    upward_grad = product_first(second_normed, grad_ffup)
    grad_second = lax.psum(grad_second, "tp")
    second_pulled = second_pull(grad_second)
    mlp_grads = (
        lax.psum_scatter(gating_grad, ("fsdp", "ctx"), scatter_dimension=0, tiled=True),
        lax.psum_scatter(upward_grad, ("fsdp", "ctx"), scatter_dimension=0, tiled=True),
        lax.psum_scatter(downward_grad, ("fsdp", "ctx"), scatter_dimension=0, tiled=True),
        lax.psum_scatter(second_pulled[1], ("fsdp", "ctx"), scatter_dimension=0, tiled=True),
        lax.psum_scatter(second_pulled[2], ("fsdp", "ctx"), scatter_dimension=0, tiled=True),
    )
    grad_middle = upstream.astype(jnp.float32) + second_pulled[0]
    back_query, back_key, back_value, back_gate, back_out = (
        full_query,
        full_key,
        full_value,
        full_gate,
        full_out,
    )
    grad_branch = grad_middle.astype(jnp.bfloat16)
    grad_gated = product(grad_branch, back_out)
    out_grad = product_first(grad_branch, gated_out)
    gate_part, mixer_part = gate_pull(grad_gated)
    grad_gate = gate_part.astype(jnp.bfloat16)
    grad_mixer = mixer_part.astype(jnp.bfloat16).reshape(value_shape)
    mixer_float = grad_mixer.astype(jnp.float32)
    grad_weights = jnp.einsum(
        "bthe,bshe->bhts", grad_mixer, value_block, preferred_element_type=jnp.float32
    )
    grad_scores = (grad_weights * score_scale * decay_table).astype(jnp.bfloat16)
    pulled_state = jnp.einsum(
        "bthd,bthe->bhde", query_float * growth, mixer_float, precision=PRECISE
    )
    returned = carried_in((through, pulled_state), "ctx", combine, (no_decay, no_state), True)
    from_later = returned[1]
    grad_query = jnp.einsum(
        "bhts,bshd->bthd", grad_scores, key_block, preferred_element_type=jnp.float32
    )
    grad_query = grad_query + growth * jnp.einsum(
        "bthe,bhde->bthd", mixer_float, incoming, precision=PRECISE
    )
    grad_query = grad_query.astype(jnp.bfloat16).reshape(row_count, -1)
    grad_key = jnp.einsum(
        "bhts,bthd->bshd", grad_scores, query_block, preferred_element_type=jnp.float32
    )
    grad_key = grad_key + keeping * jnp.einsum(
        "bshe,bhde->bshd", value_float, from_later, precision=PRECISE
    )
    grad_key = grad_key.astype(jnp.bfloat16).reshape(row_count, -1)
    grad_value = jnp.einsum(
        "bhts,bthe->bshe", weights, grad_mixer, preferred_element_type=jnp.float32
    )
    grad_value = grad_value + keeping * jnp.einsum(
        "bshd,bhde->bshe", key_float, from_later, precision=PRECISE
    )
    grad_value = grad_value.astype(jnp.bfloat16).reshape(row_count, -1)
    grad_normed = product_last(grad_query, back_query) + product_last(grad_key, back_key)
    grad_normed = (
        grad_normed + product_last(grad_value, back_value) + product_last(grad_gate, back_gate)
    )
    query_grad = product_first(normed, grad_query)
    key_grad = product_first(normed, grad_key)
    value_grad = product_first(normed, grad_value)
    gate_grad = product_first(normed, grad_gate)
    grad_normed = lax.psum(grad_normed, "tp")
    first_pulled = norm_pull(grad_normed)
    grad_tokens = (grad_middle + first_pulled[0]).astype(jnp.bfloat16).reshape(tokens.shape)
    mixer_grads = (
        lax.psum_scatter(query_grad, ("fsdp", "ctx"), scatter_dimension=0, tiled=True),
        lax.psum_scatter(key_grad, ("fsdp", "ctx"), scatter_dimension=0, tiled=True),
        lax.psum_scatter(value_grad, ("fsdp", "ctx"), scatter_dimension=0, tiled=True),
        lax.psum_scatter(gate_grad, ("fsdp", "ctx"), scatter_dimension=0, tiled=True),
        lax.psum_scatter(out_grad, ("fsdp", "ctx"), scatter_dimension=0, tiled=True),
        lax.psum_scatter(first_pulled[1], ("fsdp", "ctx"), scatter_dimension=0, tiled=True),
        lax.psum_scatter(first_pulled[2], ("fsdp", "ctx"), scatter_dimension=0, tiled=True),
    )
    return (
        output,
        grad_tokens,
        mixer_grads[0],
        mixer_grads[1],
        mixer_grads[2],
        mixer_grads[3],
        mixer_grads[4],
        mixer_grads[5],
        mixer_grads[6],
        mlp_grads[0],
        mlp_grads[1],
        mlp_grads[2],
        mlp_grads[3],
        mlp_grads[4],
    )


def solution(mesh):
    placed = (
        P("fsdp", "ctx", None),
        P("fsdp", "ctx", "tp"),
        P(("fsdp", "ctx"), "tp"),
        P(("fsdp", "ctx"), "tp"),
        P(("fsdp", "ctx"), "tp"),
        P(("fsdp", "ctx"), "tp"),
        P(("fsdp", "ctx"), "tp"),
        P(("fsdp", "ctx")),
        P(("fsdp", "ctx")),
        P(("fsdp", "ctx"), "tp"),
        P(("fsdp", "ctx"), "tp"),
        P(("fsdp", "ctx"), "tp"),
        P(("fsdp", "ctx")),
        P(("fsdp", "ctx")),
        P("fsdp", "ctx", None),
    )
    return jax.shard_map(
        shards,
        mesh=mesh,
        in_specs=placed,
        out_specs=(
            P("fsdp", "ctx", None),
            P("fsdp", "ctx", None),
            P(("fsdp", "ctx"), "tp"),
            P(("fsdp", "ctx"), "tp"),
            P(("fsdp", "ctx"), "tp"),
            P(("fsdp", "ctx"), "tp"),
            P(("fsdp", "ctx"), "tp"),
            P(("fsdp", "ctx")),
            P(("fsdp", "ctx")),
            P(("fsdp", "ctx"), "tp"),
            P(("fsdp", "ctx"), "tp"),
            P(("fsdp", "ctx"), "tp"),
            P(("fsdp", "ctx")),
            P(("fsdp", "ctx")),
        ),
        check_vma=False,
    )
```

profile of v0, /device:TPU:14, one launch (start us, length us, event | category | flops | bytes accessed | tf_op | source)
XLA Modules:
  0.0 2046.7 jit_solution(9542430052227768201)
XLA Ops:
  10.1 16.7 all-gather.2
  27.5 20.2 all-gather.3
  50.5 9.0 all-gather.23.cloned.1.call-done
  59.5 2.3 convolution_convert_fusion.4
  62.0 70.6 %all-gather.19.cloned.1.call-done = bf16[2048,1024]{1,0:T(8,128)(2,1)} async-done(((bf16[256,1024]{1,0:T(8,128)(2,1)}), bf16[2048,1024]{1,0:T(8,128)(2,1)}) %all-gather.19.cloned.1.call-update) | async-done | bytes 4194320 | tf_op jit(solution)/shard_map/all_gather | solution.py:91
  132.6 3.5 convolution_convert_fusion.2
  139.7 8.4 all_gather.60
  148.3 34.5 %all-gather.21.cloned.1.call-done = bf16[2048,512]{1,0:T(8,128)(2,1)} async-done(((bf16[256,512]{1,0:T(8,128)(2,1)}), bf16[2048,512]{1,0:T(8,128)(2,1)}) %all-gather.21.cloned.1.call-update) | async-done | bytes 2097168 | tf_op jit(solution)/shard_map/all_gather | solution.py:89
  182.9 2.4 convolution_convert_fusion.5
  187.1 75.5 %all-gather.33.cloned.1.call-done = f32[8,256,512]{2,1,0:T(8,128)} async-done(((f32[2,256,512]{2,1,0:T(8,128)}), f32[8,256,512]{2,1,0:T(8,128)}) %all-gather.33.cloned.1.call-update) | async-done | bytes 4194320 | tf_op jit(solution)/shard_map/all_gather | solution.py:20
  262.7 1.6 while.26
  264.3 3.5 bitcast_reduce_fusion
  272.1 65.0 %all-gather.17.cloned.1.call-done = bf16[2048,1024]{1,0:T(8,128)(2,1)} async-done(((bf16[256,1024]{1,0:T(8,128)(2,1)}), bf16[2048,1024]{1,0:T(8,128)(2,1)}) %all-gather.17.cloned.1.call-update) | async-done | bytes 4194320 | tf_op jit(solution)/shard_map/all_gather | solution.py:92
  337.1 5.0 multiply_convert_fusion.1
  342.2 68.3 %all-gather.25.cloned.1.call-done = bf16[2048,1024]{1,0:T(8,128)(2,1)} async-done(((bf16[256,1024]{1,0:T(8,128)(2,1)}), bf16[2048,1024]{1,0:T(8,128)(2,1)}) %all-gather.25.cloned.1.call-update) | async-done | bytes 4194320 | tf_op jit(solution)/shard_map/all_gather | solution.py:93
  410.4 4.8 fusion.109
  416.7 17.6 all-gather.4
  434.3 19.5 all-gather.5
  453.8 30.3 %all-gather.31.cloned.1.call-done = bf16[2048,1024]{1,0:T(8,128)(2,1)} async-done(((bf16[256,1024]{1,0:T(8,128)(2,1)}), bf16[2048,1024]{1,0:T(8,128)(2,1)}) %all-gather.31.cloned.1.call-update) | async-done | bytes 4194320 | tf_op jit(solution)/shard_map/all_gather | solution.py:147
  484.1 4.4 fusion.58
  488.5 48.3 %all-reduce.10.cloned.1.call-done = f32[256,2048]{1,0:T(8,128)} async-done(((f32[256,2048]{1,0:T(8,128)}), f32[256,2048]{1,0:T(8,128)}) %all-reduce.10.cloned.1.call-update) | async-done | bytes 2097168 | tf_op jit(solution)/shard_map/psum | solution.py:143
  536.8 1.9 fusion.107
  540.5 71.0 %all-gather.29.cloned.1.call-done = bf16[2048,1024]{1,0:T(8,128)(2,1)} async-done(((bf16[256,1024]{1,0:T(8,128)(2,1)}), bf16[2048,1024]{1,0:T(8,128)(2,1)}) %all-gather.29.cloned.1.call-update) | async-done | bytes 4194320 | tf_op jit(solution)/shard_map/all_gather | solution.py:146
  611.5 4.6 convolution_convert_fusion
  616.0 68.8 %all-gather.27.cloned.1.call-done = bf16[2048,1024]{1,0:T(8,128)(2,1)} async-done(((bf16[256,1024]{1,0:T(8,128)(2,1)}), bf16[2048,1024]{1,0:T(8,128)(2,1)}) %all-gather.27.cloned.1.call-update) | async-done | bytes 4194320 | tf_op jit(solution)/shard_map/all_gather | solution.py:145
  684.8 5.0 fusion.37
  692.7 2.8 convolution_add_fusion.1
  695.5 50.4 %all-reduce.12.cloned.1.call-done = f32[256,2048]{1,0:T(8,128)} async-done(((f32[256,2048]{1,0:T(8,128)}), f32[256,2048]{1,0:T(8,128)}) %all-reduce.12.cloned.1.call-update) | async-done | bytes 2097168 | tf_op jit(solution)/shard_map/psum | solution.py:175
  746.0 2.5 multiply_reduce_fusion
  750.5 1.6 copy-done.47
  753.1 2.9 fusion.73
  756.0 2.5 copy.142
  758.5 1.8 multiply_reduce_fusion.3
  763.9 5.4 fusion.89
  773.2 2.1 fusion.111
  775.3 2.7 fusion.113
  778.1 64.8 %all-gather.35.cloned.1.call-done = f32[8,256,512]{2,1,0:T(8,128)} async-done(((f32[2,256,512]{2,1,0:T(8,128)}), f32[8,256,512]{2,1,0:T(8,128)}) %all-gather.35.cloned.1.call-update) | async-done | bytes 4194320 | tf_op jit(solution)/shard_map/all_gather | solution.py:20
  844.0 6.9 while.27
  844.7 2.8 bitcast_add_fusion.8
  848.1 2.8 bitcast_add_fusion.8
  850.9 2.3 fusion.33
  854.4 3.7 fusion.112
  858.7 2.2 fusion.1
  860.9 6.4 convolution_bitcast_fusion
  867.4 2.9 fusion.97
  871.3 2.9 fusion.95
  874.5 6.4 fusion.91
  881.0 6.0 fusion.115
  887.1 5.9 fusion.114
  893.0 5.8 fusion.99
  898.9 5.7 fusion.93
  906.5 43.3 %all-reduce.14.cloned.1.call-done = (f32[256,2048]{1,0:T(8,128)}, f32[256,2048]{1,0:T(8,128)}) async-done(((f32[256,2048]{1,0:T(8,128)}, f32[256,2048]{1,0:T(8,128)}), (f32[256,2048]{1,0:T(8,128)}, f32[256,2048]{1,0:T(8,128)})) %all-reduce.14.cloned.1.call-update) | async-done | bytes 4194320 | tf_op jit(solution)/shard_map/psum | solution.py:163
  949.7 2.3 fusion.105
  953.0 33.8 %all-reduce.4 = (f32[2048]{0:T(1024)S(1)}, f32[2048]{0:T(1024)S(1)}, f32[2048]{0:T(1024)S(1)}, f32[2048]{0:T(1024)S(1)}) all-reduce(f32[2048]{0:T(1024)S(1)} %get-tuple-element.218, f32[2048]{0:T(1024)S(1)} %get-tuple-element.221, f32[2048]{0:T(1024)S(1)} %get-tuple-element.216, ...), channel_id=9, replica_groups=mesh['fsdp'=2,'ctx'=4,'tp'=4] {'fsdp','ctx'}, use_global_device_ids=true, to_apply=%region_28.29.clone | all-reduce | flops 8192 | bytes 65536
  989.4 5.6 fusion.52
  994.9 106.9 %reduce-scatter.23.cloned.1.call-done = f32[256,1024]{0,1:T(8,128)} async-done(((f32[2048,1024]{0,1:T(8,128)}), f32[256,1024]{0,1:T(8,128)}) %reduce-scatter.23.cloned.1.call-update) | async-done | bytes 1048592 | tf_op jit(solution)/shard_map/reduce_scatter | solution.py:180
  1101.8 2.5 copy.130
  1104.3 90.2 %reduce-scatter.9.cloned.1.call-done = f32[256,512]{1,0:T(8,128)} async-done(((f32[2048,512]{1,0:T(8,128)}), f32[256,512]{1,0:T(8,128)}) %reduce-scatter.9.cloned.1.call-update) | async-done | bytes 524304 | tf_op jit(solution)/shard_map/reduce_scatter | solution.py:241
  1194.5 92.0 %reduce-scatter.11.cloned.1.call-done = f32[256,512]{1,0:T(8,128)} async-done(((f32[2048,512]{1,0:T(8,128)}), f32[256,512]{1,0:T(8,128)}) %reduce-scatter.11.cloned.1.call-update) | async-done | bytes 524304 | tf_op jit(solution)/shard_map/reduce_scatter | solution.py:242
  1286.6 149.9 %reduce-scatter.21.cloned.1.call-done = f32[256,1024]{1,0:T(8,128)} async-done(((f32[2048,1024]{1,0:T(8,128)}), f32[256,1024]{1,0:T(8,128)}) %reduce-scatter.21.cloned.1.call-update) | async-done | bytes 1048592 | tf_op jit(solution)/shard_map/reduce_scatter | solution.py:179
  1436.5 150.7 %reduce-scatter.19.cloned.1.call-done = f32[256,1024]{1,0:T(8,128)} async-done(((f32[2048,1024]{1,0:T(8,128)}), f32[256,1024]{1,0:T(8,128)}) %reduce-scatter.19.cloned.1.call-update) | async-done | bytes 1048592 | tf_op jit(solution)/shard_map/reduce_scatter | solution.py:178
  1587.2 150.8 %reduce-scatter.17.cloned.1.call-done = f32[256,1024]{1,0:T(8,128)} async-done(((f32[2048,1024]{1,0:T(8,128)}), f32[256,1024]{1,0:T(8,128)}) %reduce-scatter.17.cloned.1.call-update) | async-done | bytes 1048592 | tf_op jit(solution)/shard_map/reduce_scatter | solution.py:245
  1738.0 150.6 %reduce-scatter.15.cloned.1.call-done = f32[256,1024]{1,0:T(8,128)} async-done(((f32[2048,1024]{1,0:T(8,128)}), f32[256,1024]{1,0:T(8,128)}) %reduce-scatter.15.cloned.1.call-update) | async-done | bytes 1048592 | tf_op jit(solution)/shard_map/reduce_scatter | solution.py:244
  1888.6 150.8 %reduce-scatter.13.cloned.1.call-done = f32[256,1024]{1,0:T(8,128)} async-done(((f32[2048,1024]{1,0:T(8,128)}), f32[256,1024]{1,0:T(8,128)}) %reduce-scatter.13.cloned.1.call-update) | async-done | bytes 1048592 | tf_op jit(solution)/shard_map/reduce_scatter | solution.py:243
  (222 shorter events, 44.6 us)
Async XLA Ops:
  7.2 42.6 %copy-start = (bf16[1,256,2048]{2,1,0:T(8,128)(2,1)S(1)}, bf16[1,256,2048]{2,1,0:T(8,128)(2,1)}, u32[]{:S(2)}) copy-start(bf16[1,256,2048]{2,1,0:T(8,128)(2,1)} %param.19) | copy-start | bytes 3145732
  7.2 52.3 %all-gather.23.cloned.1.call-start = ((), (), s32[]{:S(2)}) async-start(), calls=%async_computation.11 | async-start | bytes 2359296 | tf_op jit(solution)/shard_map/all_gather | solution.py:90
  7.9 124.7 %all-gather.19.cloned.1.call-start = ((), (), s32[]{:S(2)}) async-start(), calls=%async_computation.9 | async-start | bytes 4718592 | tf_op jit(solution)/shard_map/all_gather | solution.py:91
  8.7 174.2 %all-gather.21.cloned.1.call-start = ((), (), s32[]{:S(2)}) async-start(), calls=%async_computation.10 | async-start | bytes 2359296 | tf_op jit(solution)/shard_map/all_gather | solution.py:89
  9.4 253.2 %all-gather.33.cloned.1.call-start = ((), (), s32[]{:S(2)}) async-start(), calls=%async_computation.26 | async-start | bytes 5242880 | tf_op jit(solution)/shard_map/all_gather | solution.py:20
  50.5 11.4 copy-start.41
  61.9 123.5 %copy-start.32 = (bf16[256,512]{1,0:T(8,128)(2,1)}, bf16[256,512]{1,0:T(8,128)(2,1)S(1)}, u32[]{:S(2)}) copy-start(bf16[256,512]{1,0:T(8,128)(2,1)S(1)} %convolution_convert_fusion.4) | copy-start | bytes 786436
  62.0 74.1 %copy-start.22 = (bf16[256,512]{0,1:T(8,128)(2,1)}, bf16[256,512]{0,1:T(8,128)(2,1)S(1)}, u32[]{:S(2)}) copy-start(bf16[256,512]{0,1:T(8,128)(2,1)S(1)} %copy.173) | copy-start | bytes 786436
  136.1 49.6 %copy-start.17 = (bf16[256,1024]{1,0:T(8,128)(2,1)}, bf16[256,1024]{1,0:T(8,128)(2,1)S(1)}, u32[]{:S(2)}) copy-start(bf16[256,1024]{1,0:T(8,128)(2,1)S(1)} %convolution_convert_fusion.2) | copy-start | bytes 1572868
  137.7 199.4 %all-gather.17.cloned.1.call-start = ((), (), s32[]{:S(2)}) async-start(), calls=%async_computation.8 | async-start | bytes 4718592 | tf_op jit(solution)/shard_map/all_gather | solution.py:92
  138.3 272.1 %all-gather.25.cloned.1.call-start = ((), (), s32[]{:S(2)}) async-start(), calls=%async_computation.12 | async-start | bytes 4718592 | tf_op jit(solution)/shard_map/all_gather | solution.py:93
  138.9 345.2 %all-gather.31.cloned.1.call-start = ((), (), s32[]{:S(2)}) async-start(), calls=%async_computation.16 | async-start | bytes 4718592 | tf_op jit(solution)/shard_map/all_gather | solution.py:147
  139.6 397.2 %all-reduce.10.cloned.1.call-start = ((), (), s32[]{:S(2)}) async-start(), calls=%async_computation.13 | async-start | bytes 4194304 | tf_op jit(solution)/shard_map/psum | solution.py:143
  148.3 37.1 %copy-start.43 = (f32[2,256]{1,0:T(2,128)}, f32[2,256]{1,0:T(2,128)S(1)}, u32[]{:S(2)}) copy-start(f32[2,256]{1,0:T(2,128)S(1)} %bitcast_add_fusion.3) | copy-start | bytes 6148
  185.7 76.9 %copy-start.30 = (bf16[2,256,256]{2,1,0:T(8,128)(2,1)}, bf16[2,256,256]{2,1,0:T(8,128)(2,1)S(1)}, u32[]{:S(2)}) copy-start(bf16[2,256,256]{2,1,0:T(8,128)(2,1)S(1)} %fusion.31) | copy-start | bytes 786436
  264.3 3.7 copy-start.2
  264.3 3.7 copy-start.45
  267.8 2.9 copy-start.4
  270.8 66.3 %copy-start.34 = (f32[256,1024]{1,0:T(8,128)S(1)}, f32[256,1024]{1,0:T(8,128)}, u32[]{:S(2)}) copy-start(f32[256,1024]{1,0:T(8,128)} %copy.141) | copy-start | bytes 3145732
  342.2 73.1 %copy-start.38 = (bf16[256,1024]{1,0:T(8,128)(2,1)}, bf16[256,1024]{1,0:T(8,128)(2,1)S(1)}, u32[]{:S(2)}) copy-start(bf16[256,1024]{1,0:T(8,128)(2,1)S(1)} %get-tuple-element.261) | copy-start | bytes 1572868
  415.2 19.1 copy-start.50
  415.3 68.9 %copy-start.9 = (bf16[1,256,2048]{2,1,0:T(8,128)(2,1)S(1)}, bf16[1,256,2048]{2,1,0:T(8,128)(2,1)}, u32[]{:S(2)}) copy-start(bf16[1,256,2048]{2,1,0:T(8,128)(2,1)} %param.33) | copy-start | bytes 3145732
  415.3 196.2 %all-gather.29.cloned.1.call-start = ((), (), s32[]{:S(2)}) async-start(), calls=%async_computation.15 | async-start | bytes 4718592 | tf_op jit(solution)/shard_map/all_gather | solution.py:146
  416.0 268.8 %all-gather.27.cloned.1.call-start = ((), (), s32[]{:S(2)}) async-start(), calls=%async_computation.14 | async-start | bytes 4718592 | tf_op jit(solution)/shard_map/all_gather | solution.py:145
  416.6 329.3 %all-reduce.12.cloned.1.call-start = ((), (), s32[]{:S(2)}) async-start(), calls=%async_computation.17 | async-start | bytes 4194304 | tf_op jit(solution)/shard_map/psum | solution.py:175
  684.8 5.0 copy-start.48
  689.8 2.9 copy-start.21
  695.5 147.4 %all-gather.35.cloned.1.call-start = ((), (), s32[]{:S(2)}) async-start(), calls=%async_computation.27 | async-start | bytes 5242880 | tf_op jit(solution)/shard_map/all_gather | solution.py:20
  746.0 2.5 copy-start.11
  748.4 3.6 copy-start.47
  749.7 2.7 copy-start.35
  749.7 3.0 copy-start.36
  749.7 3.3 copy-start.37
  749.7 3.4 copy-start.52
  750.5 5.5 copy-start.16
  758.5 1.9 copy-start.5
  758.5 2.2 copy-start.8
  763.6 186.2 %all-reduce.14.cloned.1.call-start = ((), (), s32[]{:S(2)}) async-start(), calls=%async_computation.28 | async-start | bytes 8388608 | tf_op jit(solution)/shard_map/psum | solution.py:163
  763.8 5.5 copy-start.13
  763.8 5.4 copy-start.18
  763.9 5.4 copy-start.44
  769.3 1.7 copy-start.31
  769.7 2.6 copy-start.3
  771.0 2.2 copy-start.27
  772.3 3.0 copy-start.46
  773.2 2.1 copy-start.40
  850.9 2.3 copy-start.1
  850.9 2.3 copy-start.20
  850.9 2.3 copy-start.33
  853.3 4.9 copy-start.24
  854.4 3.8 copy-start.26
  854.4 3.8 copy-start.14
  854.4 3.8 copy-start.28
  854.4 4.3 copy-start.29
  860.9 240.9 %reduce-scatter.23.cloned.1.call-start = ((), (), s32[]{:S(2)}) async-start(), calls=%async_computation.25 | async-start | bytes 9437184 | tf_op jit(solution)/shard_map/reduce_scatter | solution.py:180
  867.4 327.2 %reduce-scatter.9.cloned.1.call-start = ((), (), s32[]{:S(2)}) async-start(), calls=%async_computation.18 | async-start | bytes 4718592 | tf_op jit(solution)/shard_map/reduce_scatter | solution.py:241
  870.4 416.2 %reduce-scatter.11.cloned.1.call-start = ((), (), s32[]{:S(2)}) async-start(), calls=%async_computation.19 | async-start | bytes 4718592 | tf_op jit(solution)/shard_map/reduce_scatter | solution.py:242
  874.2 562.3 %reduce-scatter.21.cloned.1.call-start = ((), (), s32[]{:S(2)}) async-start(), calls=%async_computation.24 | async-start | bytes 9437184 | tf_op jit(solution)/shard_map/reduce_scatter | solution.py:179
  881.0 706.2 %reduce-scatter.19.cloned.1.call-start = ((), (), s32[]{:S(2)}) async-start(), calls=%async_computation.23 | async-start | bytes 9437184 | tf_op jit(solution)/shard_map/reduce_scatter | solution.py:178
  887.0 851.0 %reduce-scatter.17.cloned.1.call-start = ((), (), s32[]{:S(2)}) async-start(), calls=%async_computation.22 | async-start | bytes 9437184 | tf_op jit(solution)/shard_map/reduce_scatter | solution.py:245
  893.0 995.6 %reduce-scatter.15.cloned.1.call-start = ((), (), s32[]{:S(2)}) async-start(), calls=%async_computation.21 | async-start | bytes 9437184 | tf_op jit(solution)/shard_map/reduce_scatter | solution.py:244
  898.8 1140.6 %reduce-scatter.13.cloned.1.call-start = ((), (), s32[]{:S(2)}) async-start(), calls=%async_computation.20 | async-start | bytes 9437184 | tf_op jit(solution)/shard_map/reduce_scatter | solution.py:243
  904.6 47.4 %copy-start.42 = (f32[256]{0:T(256)S(1)}, f32[256]{0:T(256)}, u32[]{:S(2)}) copy-start(f32[256]{0:T(256)} %copy-done.41) | copy-start | bytes 3076
  949.7 2.3 copy-start.7
  (10 other events, 12.3 us)
Sparse Core Ops, SparseCore 0:
  10.1 49.3 all-gather.22
  61.6 70.9 all-gather.18
  134.8 48.0 all-gather.20
  184.9 77.6 all-gather.32
  264.6 72.5 all-gather.16
  339.1 71.3 all-gather.24
  412.6 71.4 all-gather.30
  486.5 50.2 all-reduce.9
  538.9 72.4 all-gather.28
  613.4 71.3 all-gather.26
  695.6 50.2 all-reduce.11
  763.7 79.1 all-gather.34
  861.0 88.7 all-reduce.13
  953.2 148.5 reduce-scatter.22
  1105.9 88.6 reduce-scatter.8
  1198.6 87.9 reduce-scatter.10
  1290.6 145.8 reduce-scatter.20
  1440.6 146.5 reduce-scatter.18
  1591.4 146.5 reduce-scatter.16
  1742.0 146.5 reduce-scatter.14
  1892.8 146.5 reduce-scatter.12
where the time goes:
time: 2060 us; the launch traced here: 2050 us
  waiting for transfers between devices  1750 us (85%)
  blocking collectives  116 us (6%)
  matrix products  112 us (5%)
  other arithmetic  27.1 us (1%)
  local copies, waits for them, and re-layouts  26.5 us (1%)
    reduce_scatter x1, waiting for transfers between devices, shards(): lax.psum_scatter(out_grad, ('fsdp', 'ctx'), scatter_dimension=0, tiled=True)  151 us
    reduce_scatter x1, waiting for transfers between devices, shards(): lax.psum_scatter(value_grad, ('fsdp', 'ctx'), scatter_dimension=0, tiled=...  151 us
    reduce_scatter x1, waiting for transfers between devices, shards(): lax.psum_scatter(gating_grad, ('fsdp', 'ctx'), scatter_dimension=0, tiled...  151 us
    reduce_scatter x1, waiting for transfers between devices, shards(): lax.psum_scatter(gate_grad, ('fsdp', 'ctx'), scatter_dimension=0, tiled=T...  151 us
    reduce_scatter x1, waiting for transfers between devices, shards(): lax.psum_scatter(upward_grad, ('fsdp', 'ctx'), scatter_dimension=0, tiled...  150 us
    all_gather x2, waiting for transfers between devices, carried_in(): gathered = jax.tree.map(lambda a: lax.all_gather(a, axis), part)  140 us
    reduce_scatter x1, waiting for transfers between devices, shards(): lax.psum_scatter(downward_grad, ('fsdp', 'ctx'), scatter_dimension=0, til...  107 us
    reduce_scatter x1, waiting for transfers between devices, shards(): lax.psum_scatter(key_grad, ('fsdp', 'ctx'), scatter_dimension=0, tiled=True)  92 us
  transfers between devices with their start and end apart: 21, of which 21 were waited for; matrix products, arithmetic and copies ran while one was open for 6% of the time, Pallas kernels for 0%

commit v1 on v0

v1 whole, which is shorter than its diff:
```python
import functools

import jax
import jax.numpy as jnp
from jax import lax
from jax.experimental import pallas as pl
from jax.experimental.pallas import tpu as pltpu
from jax.sharding import PartitionSpec as P

KEY = 256
HEAD_V = 512
EPSILON = 1e-05
MESH = pl.DeviceIdType.MESH
ANY = pl.BlockSpec(memory_space=pl.ANY)
VMEM = pl.BlockSpec(memory_space=pltpu.VMEM)
BF = jnp.bfloat16
F32 = jnp.float32


def dot(a, b, dims):
    return lax.dot_general(a, b, (dims, ((), ())), preferred_element_type=F32)


def nn(a, b):
    return dot(a, b, ((1,), (0,)))


def nt(a, b):
    return dot(a, b, ((1,), (1,)))


def tn(a, b):
    return dot(a, b, ((0,), (0,)))


class Place:
    def __init__(self, F, C, T):
        self.F, self.C, self.T = F, C, T
        self.f = lax.axis_index("fsdp")
        self.z = lax.axis_index("ctx")
        self.t = lax.axis_index("tp")
        self.lo = lax.rem(self.t, 2)
        self.hi = self.t // 2
        self.near = self.t + 1 - 2 * self.lo
        self.far = lax.rem(self.t + 2, 4)

    def ahead(self, d):
        return lax.rem(self.z + d, self.C)

    def behind(self, d):
        return lax.rem(self.z + self.C - d, self.C)

    def fahead(self, d):
        return lax.rem(self.f + d, self.F)

    def fbehind(self, d):
        return lax.rem(self.f + self.F - d, self.F)

    def barrier(self, ctx=True, fsdp=False, tp=True):
        sem = pltpu.get_barrier_semaphore()
        peers = []
        if tp:
            peers += [{"tp": self.near}, {"tp": self.far}]
        if fsdp:
            peers += [{"fsdp": self.fahead(d)} for d in range(1, self.F)]
        if ctx:
            peers += [{"ctx": self.ahead(d)} for d in range(1, self.C)]
        for peer in peers:
            pl.semaphore_signal(sem, inc=1, device_id=peer, device_id_type=MESH)
        pl.semaphore_wait(sem, len(peers))


def remote(src, dst, ssem, rsem, peer):
    return pltpu.make_async_remote_copy(
        src_ref=src, dst_ref=dst, send_sem=ssem, recv_sem=rsem, device_id=peer, device_id_type=MESH
    )


def sem(*shape):
    return pltpu.SemaphoreType.DMA(shape)


def gather_sems(C):
    return [sem(C), sem(C), sem(C), sem(C), sem(C, 2), sem(C, 2)]


def gather_stage(pc, x, out, lsem, sems, owned=False):
    C = pc.C
    zs, zr, ys, yr, cs, cr = sems
    z, t = pc.z, pc.t
    started = []
    local = pltpu.make_async_copy(x, out.at[z, t], lsem)
    local.start()
    zc = [None] * C
    for d in range(1, C):
        zc[d] = remote(x, out.at[z, t], zs.at[d], zr.at[d], {"ctx": pc.ahead(d)})
        zc[d].start()
    yc = [None] * C
    cc = [[None, None] for _ in range(C)]
    for d in range(C):
        c = pc.behind(d)
        src = x if d == 0 else out.at[c, t]
        if d:
            zc[d].wait_recv()
        yc[d] = remote(src, out.at[c, t], ys.at[d], yr.at[d], {"tp": pc.far})
        yc[d].start()
        cc[d][0] = remote(src, out.at[c, t], cs.at[d, 0], cr.at[d, 0], {"tp": pc.near})
        cc[d][0].start()
    for d in range(C):
        c = pc.behind(d)
        yc[d].wait_recv()
        src = out.at[c, pc.far]
        cc[d][1] = remote(src, src, cs.at[d, 1], cr.at[d, 1], {"tp": pc.near})
        cc[d][1].start()
    local.wait()
    for d in range(C):
        if d:
            zc[d].wait_send()
        yc[d].wait_send()
        for j in range(2):
            cc[d][j].wait()


def share_sems():
    return [sem(3), sem(3)]


def share_stage(pc, x, out, lsem, sems):
    ss, rs = sems
    t = pc.t
    local = pltpu.make_async_copy(x, out.at[t], lsem)
    local.start()
    a = remote(x, out.at[t], ss.at[0], rs.at[0], {"tp": pc.far})
    a.start()
    b = remote(x, out.at[t], ss.at[1], rs.at[1], {"tp": pc.near})
    b.start()
    a.wait_recv()
    src = out.at[pc.far]
    c = remote(src, src, ss.at[2], rs.at[2], {"tp": pc.near})
    c.start()
    local.wait()
    a.wait_send()
    b.wait()
    c.wait()


def scatter_scratch(C, Q, W):
    return [
        pltpu.VMEM((C, 2, Q, W), BF),
        pltpu.VMEM((C, 2, Q, W), BF),
        pltpu.VMEM((C, Q, W), BF),
        pltpu.VMEM((C, Q, W), BF),
        pltpu.VMEM((C, Q, W), BF),
        pltpu.VMEM((C, Q, W), BF),
        sem(C, 2),
        sem(C, 2),
        sem(C, 2),
        sem(C),
        sem(C),
        sem(C),
        sem(C),
    ]


class Scatter:
    def __init__(self, pc, p, scratch):
        self.pc, self.p = pc, p
        (self.loc, self.buf1, self.snd2, self.buf2, self.snd3, self.buf3) = scratch[:6]
        self.ls, self.s1, self.r1, self.s2, self.r2, self.s3, self.r3 = scratch[6:]

    def start(self):
        pc, p = self.pc, self.p
        C = pc.C
        self.order = list(range(1, C)) + [0]
        self.lc, self.c1 = {}, {}
        for d in self.order:
            c = pc.ahead(d)
            for j in range(2):
                hi = 1 - pc.hi if j == 0 else pc.hi
                cp = remote(
                    p.at[c, hi * 2 + 1 - pc.lo],
                    self.buf1.at[d, j],
                    self.s1.at[d, j],
                    self.r1.at[d, j],
                    {"tp": pc.near},
                )
                cp.start()
                self.c1[d, j] = cp
                lc = pltpu.make_async_copy(
                    p.at[c, hi * 2 + pc.lo], self.loc.at[d, j], self.ls.at[d, j]
                )
                lc.start()
                self.lc[d, j] = lc

    def finish(self):
        pc = self.pc
        c2, c3 = {}, {}
        for d in self.order:
            self.lc[d, 0].wait()
            self.c1[d, 0].wait_recv()
            self.snd2[d] = (self.loc[d, 0].astype(F32) + self.buf1[d, 0].astype(F32)).astype(BF)
            c2[d] = remote(
                self.snd2.at[d], self.buf2.at[d], self.s2.at[d], self.r2.at[d], {"tp": pc.far}
            )
            c2[d].start()
        total = None
        for d in self.order:
            self.lc[d, 1].wait()
            self.c1[d, 1].wait_recv()
            c2[d].wait_recv()
            part = (
                self.loc[d, 1].astype(F32)
                + self.buf1[d, 1].astype(F32)
                + self.buf2[d].astype(F32)
            )
            if d:
                self.snd3[d] = part.astype(BF)
                c3[d] = remote(
                    self.snd3.at[d],
                    self.buf3.at[d],
                    self.s3.at[d],
                    self.r3.at[d],
                    {"ctx": pc.ahead(d)},
                )
                c3[d].start()
            else:
                total = part
        for d in range(1, pc.C):
            c3[d].wait_recv()
            total = total + self.buf3[d].astype(F32)
        for d in self.order:
            self.c1[d, 0].wait_send()
            self.c1[d, 1].wait_send()
            c2[d].wait_send()
            if d:
                c3[d].wait_send()
        return total


def first_kernel(
    dims, win, wrest, vec, ld, tok, go, owin, owrest, ovec, old, otok, ogo, ls, zs, zr, xs, xr, ys, yr, cs, cr
):
    pc = Place(*dims)
    F, C, T = dims
    f, z, t = pc.f, pc.z, pc.t
    pc.barrier(True, True, True)
    pieces = [win, wrest, vec, ld]
    outs = [owin, owrest, ovec, old]

    def piece(i, dst):
        return pieces[i].at[dst] if i < 2 else pieces[i]

    def slot(i, ff, c):
        return outs[i].at[ff, c] if i < 3 else outs[i].at[c]

    acts, oacts = [tok, go], [otok, ogo]
    zc, xc, yc, cc = {}, {}, {}, {}

    def send_piece(i):
        for d in range(1, C):
            dst = pc.ahead(d)
            zc[i, d] = remote(piece(i, dst), slot(i, f, z), zs.at[i, d], zr.at[i, d], {"ctx": dst})
            zc[i, d].start()

    def send_act(i):
        for d in range(1, C):
            k = 4 + i
            zc[k, d] = remote(
                acts[i].at[t], oacts[i].at[z, t], zs.at[k, d], zr.at[k, d], {"ctx": pc.ahead(d)}
            )
            zc[k, d].start()

    def across(i, d):
        c = pc.behind(d)
        src = piece(i, z) if d == 0 else slot(i, f, c)
        for e in range(1, F):
            xc[i, d, e] = remote(
                src, slot(i, f, c), xs.at[i, d, e], xr.at[i, d, e], {"fsdp": pc.fahead(e)}
            )
            xc[i, d, e].start()

    def spread(i, d):
        c = pc.behind(d)
        src = oacts[i].at[c, t]
        yc[i, d] = remote(src, src, ys.at[i, d], yr.at[i, d], {"tp": pc.far})
        yc[i, d].start()
        cc[i, d, 0] = remote(src, src, cs.at[i, d, 0], cr.at[i, d, 0], {"tp": pc.near})
        cc[i, d, 0].start()

    def spread_on(i, d):
        c = pc.behind(d)
        yc[i, d].wait_recv()
        src = oacts[i].at[c, pc.far]
        cc[i, d, 1] = remote(src, src, cs.at[i, d, 1], cr.at[i, d, 1], {"tp": pc.near})
        cc[i, d, 1].start()

    for i in (2, 3):
        send_piece(i)
    send_act(0)
    send_piece(0)
    for i in (2, 0):
        across(i, 0)
    send_piece(1)
    send_act(1)
    across(1, 0)
    local = []
    for i in range(4):
        local.append(pltpu.make_async_copy(piece(i, z), slot(i, f, z), ls.at[i]))
    for i in range(2):
        local.append(pltpu.make_async_copy(acts[i], oacts[i].at[z], ls.at[4 + i]))
    for cp in local:
        cp.start()
    for d in range(1, C):
        zc[2, d].wait_recv()
        across(2, d)
        zc[4, d].wait_recv()
        spread(0, d)
    for d in range(1, C):
        zc[0, d].wait_recv()
        across(0, d)
    for d in range(1, C):
        spread_on(0, d)
    for d in range(1, C):
        zc[1, d].wait_recv()
        across(1, d)
        zc[5, d].wait_recv()
        spread(1, d)
    for d in range(1, C):
        spread_on(1, d)
        zc[3, d].wait_recv()
    for cp in local:
        cp.wait()
    for cp in zc.values():
        cp.wait_send()
    for cp in xc.values():
        cp.wait()
    for cp in yc.values():
        cp.wait_send()
    for cp in cc.values():
        cp.wait()


def out_kernel(dims, p, tok, gain, bias, mid, sn, x, lsem, *scratch):
    pc = Place(*dims)
    pc.barrier()
    n = len(gather_sems(pc.C))
    rs = Scatter(pc, p, scratch[n:])
    rs.start()
    total = rs.finish() + tok[...].astype(F32)
    mid[...] = total
    center = total - jnp.mean(total, axis=-1, keepdims=True)
    spread = jnp.mean(center * center, axis=-1, keepdims=True)
    x[...] = (center * lax.rsqrt(spread + EPSILON) * gain[...] + bias[...]).astype(BF)
    gather_stage(pc, x, sn, lsem, scratch[:n])


def norm_pull(values, gain, grad):
    center = values - jnp.mean(values, axis=-1, keepdims=True)
    spread = jnp.mean(center * center, axis=-1, keepdims=True)
    inv = lax.rsqrt(spread + EPSILON)
    xhat = center * inv
    g = grad * gain
    back = inv * (
        g - jnp.mean(g, axis=-1, keepdims=True) - xhat * jnp.mean(g * xhat, axis=-1, keepdims=True)
    )
    return (
        back,
        jnp.sum(grad * xhat, axis=0, keepdims=True),
        jnp.sum(grad, axis=0, keepdims=True),
    )


def mlp_kernel(
    dims, pg, pd, mid, go, gain, gm, gb, out, dgain, dbias, x, y, lsem, *scratch
):
    pc = Place(*dims)
    pc.barrier()
    n = len(gather_sems(pc.C))
    m = (len(scratch) - n - 2) // 2
    gs, ss = scratch[:n], scratch[n : n + 2]
    rg = Scatter(pc, pg, scratch[n + 2 : n + 2 + m])
    rd = Scatter(pc, pd, scratch[n + 2 + m :])
    rg.start()
    rd.start()
    back, dg, db = norm_pull(mid[...], gain[...], rg.finish())
    dgain[...] = dg
    dbias[...] = db
    grad_middle = go[...].astype(F32) + back
    gm[...] = grad_middle
    x[...] = grad_middle.astype(BF)
    gather_stage(pc, x, gb, lsem.at[0], gs)
    y[...] = (mid[...] + rd.finish()).astype(BF)
    share_stage(pc, y, out, lsem.at[1], ss)


def last_kernel(dims, p, gm, tok, gain, gt, dgain, dbias, y, lsem, s0, s1, *scratch):
    pc = Place(*dims)
    pc.barrier()
    rs = Scatter(pc, p, scratch)
    rs.start()
    back, dg, db = norm_pull(tok[...].astype(F32), gain[...], rs.finish())
    dgain[...] = dg
    dbias[...] = db
    y[...] = (gm[...] + back).astype(BF)
    share_stage(pc, y, gt, lsem, (s0, s1))


def grads_kernel(
    dims, g, v, out, vout, own, xbuf, zsnd, va, vb, vc, vd, vx, vz, ls, osem, xs, xr, zs, zr, ts, tr, vxs, vxr, vzs, vzr
):
    pc = Place(*dims)
    F, C, T = dims
    f, z = pc.f, pc.z
    pc.barrier(True, True, True)
    order = list(range(1, C)) + [0]
    loc, xc, zc = {}, {}, {}
    t0 = remote(v, vb, ts.at[0], tr.at[0], {"tp": pc.near})
    t0.start()
    for d in order:
        c = pc.ahead(d)
        for e in range(1, F):
            xc[d, e] = remote(
                g.at[pc.fahead(e), c], xbuf.at[e - 1, d], xs.at[d, e], xr.at[d, e], {"fsdp": pc.fahead(e)}
            )
            xc[d, e].start()
        loc[d] = pltpu.make_async_copy(g.at[f, c], own.at[d], ls.at[d])
        loc[d].start()
    t0.wait_recv()
    va[...] = v[...] + vb[...]
    t1 = remote(va, vc, ts.at[1], tr.at[1], {"tp": pc.far})
    t1.start()
    t1.wait_recv()
    vd[...] = va[...] + vc[...]
    vxc = {}
    for e in range(1, F):
        vxc[e] = remote(
            vd.at[pc.fahead(e)], vx.at[e - 1], vxs.at[e], vxr.at[e], {"fsdp": pc.fahead(e)}
        )
        vxc[e].start()
    vs = vd[f]
    for e in range(1, F):
        vxc[e].wait_recv()
        vs = vs + vx[e - 1]
    vxs_ref = vz.at[0]
    vxs_ref[...] = vs
    vzc = {}
    for d in range(1, C):
        vzc[d] = remote(
            vz.at[0, pc.ahead(d)], vz.at[1, d], vzs.at[d], vzr.at[d], {"ctx": pc.ahead(d)}
        )
        vzc[d].start()
    keep = None
    for d in order:
        loc[d].wait()
        total = own[d].astype(F32)
        for e in range(1, F):
            xc[d, e].wait_recv()
            total = total + xbuf[e - 1, d].astype(F32)
        zsnd[d] = total.astype(BF)
        if d:
            zc[d] = remote(
                zsnd.at[d], out.at[z], zs.at[d], zr.at[d], {"ctx": pc.ahead(d)}
            )
            zc[d].start()
        else:
            keep = pltpu.make_async_copy(zsnd.at[0], out.at[z], osem)
            keep.start()
    acc = vz[0, z]
    for d in range(1, C):
        vzc[d].wait_recv()
        acc = acc + vz[1, d]
    vout[...] = acc
    keep.wait()
    for cp in zc.values():
        cp.wait()
    for cp in xc.values():
        cp.wait_send()
    for cp in [t0, t1] + list(vxc.values()) + list(vzc.values()):
        cp.wait_send()


def params(cid):
    return pltpu.CompilerParams(collective_id=cid, has_side_effects=True)


def silu_parts(g):
    s = jax.nn.sigmoid(g)
    return g * s, s * (1.0 + g * (1.0 - s))


def shards(
    dims,
    tokens,
    log_decay,
    w_query,
    w_key,
    w_value,
    w_gate,
    w_out,
    norm1_gain,
    norm1_bias,
    w_ffgate,
    w_ffup,
    w_down,
    norm2_gain,
    norm2_bias,
    grad_out,
):
    F, C, T = dims
    S, B, W = tokens.shape
    L = S * B
    Q = L // T
    N = C * L
    R = w_query.shape[0]
    heads = log_decay.shape[2]
    halves = C // heads
    HV = HEAD_V // halves
    U = w_ffgate.shape[1] // C
    z = lax.axis_index("ctx")
    t = lax.axis_index("tp")
    scale = float(KEY) ** (-0.5)

    def cols(w, i, n):
        return w[:, i * n : (i + 1) * n]

    win = jnp.stack(
        [
            jnp.concatenate(
                [
                    cols(w_query, c // halves, KEY),
                    cols(w_key, c // halves, KEY),
                    cols(w_value, c, HV),
                    cols(w_gate, c, HV),
                ],
                axis=1,
            )
            for c in range(C)
        ]
    )
    wrest = jnp.stack(
        [
            jnp.concatenate(
                [cols(w_out, c, HV), cols(w_ffgate, c, U), cols(w_ffup, c, U), cols(w_down, c, U)],
                axis=1,
            )
            for c in range(C)
        ]
    )
    NI, NR = win.shape[2], wrest.shape[2]
    vec = jnp.stack([norm1_gain, norm1_bias, norm2_gain, norm2_bias]).astype(F32)
    vec = jnp.pad(vec, ((0, 4), (0, 0)))
    ld = jnp.pad(jnp.transpose(log_decay, (2, 0, 1)).reshape(heads, L), ((0, 8 - heads), (0, 0)))
    tok = tokens.reshape(T, Q, W)
    go = grad_out.reshape(T, Q, W)
    sds = jax.ShapeDtypeStruct
    owin, owrest, ovec, old, otok, ogo = pl.pallas_call(
        functools.partial(first_kernel, dims),
        out_shape=(
            sds((F, C, R, NI), BF),
            sds((F, C, R, NR), BF),
            sds((F, C, 8, R), F32),
            sds((C, 8, L), F32),
            sds((C, T, Q, W), BF),
            sds((C, T, Q, W), BF),
        ),
        in_specs=[ANY] * 6,
        out_specs=[ANY] * 6,
        scratch_shapes=[
            sem(6),
            sem(6, C),
            sem(6, C),
            sem(3, C, F),
            sem(3, C, F),
            sem(2, C),
            sem(2, C),
            sem(2, C, 2),
            sem(2, C, 2),
        ],
        compiler_params=params(1),
        name="k_first",
    )(win, wrest, vec, ld, tok, go)

    vecs = jnp.transpose(ovec[:, :, :4], (2, 0, 1, 3)).reshape(4, 1, W)
    gain1, bias1, gain2, bias2 = vecs[0], vecs[1], vecs[2], vecs[3]
    w_in = owin.reshape(W, NI)
    w_rest = owrest.reshape(W, NR)
    w_o, w_fg, w_fu, w_d = w_rest[:, :HV], w_rest[:, HV : HV + U], w_rest[:, HV + U : HV + 2 * U], w_rest[:, HV + 2 * U :]
    xs = otok.reshape(N, W).astype(F32)
    center = xs - jnp.mean(xs, axis=-1, keepdims=True)
    spread = jnp.mean(center * center, axis=-1, keepdims=True)
    normed = (center * lax.rsqrt(spread + EPSILON) * gain1 + bias1).astype(BF)
    proj = nn(normed, w_in).astype(BF)
    q = proj[:, :KEY].reshape(C, S, B, KEY)
    k = proj[:, KEY : 2 * KEY].reshape(C, S, B, KEY)
    v = proj[:, 2 * KEY : 2 * KEY + HV].reshape(C, S, B, HV)
    g = proj[:, 2 * KEY + HV :].reshape(C, S, B, HV).astype(F32)

    rates = lax.dynamic_index_in_dim(old, z // halves, 1, False).reshape(C, S, B)
    cum = jnp.cumsum(rates, axis=-1)
    total = cum[..., -1]
    positions = jnp.arange(B)
    causal = positions[:, None] >= positions[None, :]
    table = jnp.where(
        causal, jnp.exp(jnp.minimum(cum[..., :, None] - cum[..., None, :], 0.0)), 0.0
    )
    growth = jnp.exp(cum)[..., None]
    keeping = jnp.exp(total[..., None] - cum)[..., None]
    through = jnp.exp(total)[..., None, None]

    def ein(spec, a, b):
        return jnp.einsum(spec, a, b, preferred_element_type=F32)

    weights = (ein("cstd,csud->cstu", q, k) * scale * table).astype(BF)
    q_grown = (q.astype(F32) * growth).astype(BF)
    k_kept = (k.astype(F32) * keeping).astype(BF)
    fresh = ein("csud,csue->csde", k_kept, v)
    state = jnp.zeros_like(fresh[0])
    states = []
    for c in range(C):
        states.append(state.astype(BF))
        state = through[c] * state + fresh[c]
    states = jnp.stack(states)
    mixer = ein("cstu,csue->cste", weights, v) + ein("cstd,csde->cste", q_grown, states)

    def pair(stats):
        got = [stats]
        for j in range(1, halves):
            perm = []
            for c in range(C):
                base = c - c % halves
                perm.append((c, base + (c % halves + j) % halves))
            got.append(lax.ppermute(stats, "ctx", perm))
        return got

    mean_here = jnp.mean(mixer, axis=-1)
    dev = mixer - mean_here[..., None]
    m2_here = jnp.sum(dev * dev, axis=-1)
    got = pair(jnp.stack([mean_here, m2_here]))
    mean = sum(x[0] for x in got) / halves
    m2 = sum(x[1] + HV * (x[0] - mean) ** 2 for x in got)
    inv = lax.rsqrt(m2 / HEAD_V + EPSILON)[..., None]
    normal = (mixer - mean[..., None]) * inv
    silu, dsilu = silu_parts(g)
    gated = (silu * normal).astype(BF).reshape(N, HV)

    part = nt(gated, w_o).astype(BF).reshape(C, T, Q, W)
    mytok = lax.dynamic_index_in_dim(tok, t, 0, False)
    mygo = lax.dynamic_index_in_dim(go, t, 0, False)
    mid, sn = pl.pallas_call(
        functools.partial(out_kernel, dims),
        out_shape=(sds((Q, W), F32), sds((C, T, Q, W), BF)),
        in_specs=[ANY, VMEM, VMEM, VMEM],
        out_specs=[VMEM, ANY],
        scratch_shapes=[pltpu.VMEM((Q, W), BF), pltpu.SemaphoreType.DMA]
        + gather_sems(C)
        + scatter_scratch(C, Q, W),
        compiler_params=params(2),
        name="k_out",
    )(part, mytok, gain2, bias2)

    second = sn.reshape(N, W)
    ff_gate = nn(second, w_fg).astype(BF)
    ff_up = nn(second, w_fu).astype(BF)
    hidden, gelu_pull = jax.vjp(
        lambda a, b: jax.nn.gelu(a, approximate=True) * b, ff_gate.astype(F32), ff_up.astype(F32)
    )
    hidden = hidden.astype(BF)
    down = nt(hidden, w_d).astype(BF).reshape(C, T, Q, W)
    gout = ogo.reshape(N, W)
    grad_hidden = nn(gout, w_d)
    gfg, gfu = gelu_pull(grad_hidden)
    gfg, gfu = gfg.astype(BF), gfu.astype(BF)
    gsecond = (nt(gfg, w_fg) + nt(gfu, w_fu)).astype(BF).reshape(C, T, Q, W)
    gm, gb, out, dgain2, dbias2 = pl.pallas_call(
        functools.partial(mlp_kernel, dims),
        out_shape=(
            sds((Q, W), F32),
            sds((C, T, Q, W), BF),
            sds((T, Q, W), BF),
            sds((1, W), F32),
            sds((1, W), F32),
        ),
        in_specs=[ANY, ANY, VMEM, VMEM, VMEM],
        out_specs=[VMEM, ANY, ANY, VMEM, VMEM],
        scratch_shapes=[pltpu.VMEM((Q, W), BF), pltpu.VMEM((Q, W), BF), sem(2)]
        + gather_sems(C)
        + share_sems()
        + scatter_scratch(C, Q, W)
        + scatter_scratch(C, Q, W),
        compiler_params=params(3),
        name="k_mlp",
    )(gsecond, down, mid, mygo, gain2)
    output = out.reshape(tokens.shape)

    branch = gb.reshape(N, W)
    ggated = nn(branch, w_o).reshape(C, S, B, HV)
    ggate = (ggated * normal * dsilu).astype(BF)
    gn = ggated * silu
    sums = pair(jnp.stack([jnp.sum(gn, axis=-1), jnp.sum(gn * normal, axis=-1)]))
    s1 = sum(x[0] for x in sums)[..., None] / HEAD_V
    s2 = sum(x[1] for x in sums)[..., None] / HEAD_V
    gmixer = (inv * (gn - s1 - normal * s2)).astype(BF)
    gscores = (ein("cste,csue->cstu", gmixer, v) * scale * table).astype(BF)
    pulled = ein("cstd,cste->csde", q_grown, gmixer)
    later = jnp.zeros_like(pulled[0])
    laters = [None] * C
    for c in reversed(range(C)):
        laters[c] = later.astype(BF)
        later = through[c] * later + pulled[c]
    laters = jnp.stack(laters)
    gq = ein("cstu,csud->cstd", gscores, k) + growth * ein("cste,csde->cstd", gmixer, states)
    gk = ein("cstu,cstd->csud", gscores, q) + keeping * ein("csue,csde->csud", v, laters)
    gv = ein("cstu,cste->csue", weights, gmixer) + ein("csud,csde->csue", k_kept, laters)
    gproj = jnp.concatenate([gq.astype(BF), gk.astype(BF), gv.astype(BF), ggate], axis=-1)
    gproj = gproj.reshape(N, NI)

    gnormed = nt(gproj, w_in).astype(BF).reshape(C, T, Q, W)
    gt, dgain1, dbias1 = pl.pallas_call(
        functools.partial(last_kernel, dims),
        out_shape=(sds((T, Q, W), BF), sds((1, W), F32), sds((1, W), F32)),
        in_specs=[ANY, VMEM, VMEM, VMEM],
        out_specs=[ANY, VMEM, VMEM],
        scratch_shapes=[pltpu.VMEM((Q, W), BF), pltpu.SemaphoreType.DMA]
        + share_sems()
        + scatter_scratch(C, Q, W),
        compiler_params=params(4),
        name="k_last",
    )(gnormed, gm, mytok, gain1)
    grad_tokens = gt.reshape(tokens.shape)

    grads = jnp.concatenate(
        [
            tn(normed, gproj).astype(BF),
            tn(branch, gated).astype(BF),
            tn(second, gfg).astype(BF),
            tn(second, gfu).astype(BF),
            tn(gout, hidden).astype(BF),
        ],
        axis=1,
    ).reshape(F, C, R, NI + NR)
    vpart = jnp.concatenate([dgain1, dbias1, dgain2, dbias2, jnp.zeros((4, W), F32)], axis=0)
    vpart = jnp.transpose(vpart.reshape(8, F, C, R), (1, 2, 0, 3))
    NG = NI + NR
    gsum, vsum = pl.pallas_call(
        functools.partial(grads_kernel, dims),
        out_shape=(sds((C, R, NG), BF), sds((8, R), F32)),
        in_specs=[ANY, VMEM],
        out_specs=[ANY, VMEM],
        scratch_shapes=[
            pltpu.VMEM((C, R, NG), BF),
            pltpu.VMEM((F - 1, C, R, NG), BF),
            pltpu.VMEM((C, R, NG), BF),
            pltpu.VMEM((F, C, 8, R), F32),
            pltpu.VMEM((F, C, 8, R), F32),
            pltpu.VMEM((F, C, 8, R), F32),
            pltpu.VMEM((F, C, 8, R), F32),
            pltpu.VMEM((F - 1, C, 8, R), F32),
            pltpu.VMEM((2, C, 8, R), F32),
            sem(C),
            pltpu.SemaphoreType.DMA,
            sem(C, F),
            sem(C, F),
            sem(C),
            sem(C),
            sem(2),
            sem(2),
            sem(F),
            sem(F),
            sem(C),
            sem(C),
        ],
        compiler_params=params(5),
        name="k_grads",
    )(grads, vpart)

    def by_head(lo):
        x = gsum[:, :, lo : lo + KEY].astype(F32).reshape(heads, halves, R, KEY).sum(axis=1)
        return jnp.transpose(x, (1, 0, 2)).reshape(R, heads * KEY)

    def side(lo, n):
        return jnp.transpose(gsum[:, :, lo : lo + n].astype(F32), (1, 0, 2)).reshape(R, C * n)

    return (
        output,
        grad_tokens,
        by_head(0),
        by_head(KEY),
        side(2 * KEY, HV),
        side(2 * KEY + HV, HV),
        side(NI, HV),
        vsum[0],
        vsum[1],
        side(NI + HV, U),
        side(NI + HV + U, U),
        side(NI + HV + 2 * U, U),
        vsum[2],
        vsum[3],
    )


def solution(mesh):
    dims = (mesh.shape["fsdp"], mesh.shape["ctx"], mesh.shape["tp"])
    rows, vec = P(("fsdp", "ctx"), "tp"), P(("fsdp", "ctx"))
    acts = P("fsdp", "ctx", None)
    return jax.shard_map(
        functools.partial(shards, dims),
        mesh=mesh,
        in_specs=(acts, P("fsdp", "ctx", "tp"), rows, rows, rows, rows, rows, vec, vec, rows, rows, rows, vec, vec, acts),
        out_specs=(acts, acts, rows, rows, rows, rows, rows, vec, vec, rows, rows, rows, vec, vec),
        check_vma=False,
    )
```

time: 2060 us -> 781 us (0.38)
  waiting for transfers between devices: 1750 us -> 0.01 us
  Pallas kernels: 0 us -> 596 us
  blocking collectives: 116 us -> 0 us
  matrix products: 112 us -> 66.2 us
  local copies, waits for them, and re-layouts: 26.5 us -> 71 us
    reduce_scatter x8 -> x0, waiting for transfers between devices: 1040 us -> none  [the longest x1 151 us: shards(): lax.psum_scatter(out_grad, ('fsdp', 'ctx'), scatter_dimension=0, tiled=True)]
    pallas_call x0 -> x5, Pallas kernels: none -> 596 us  [the longest x1 189 us: shards(): pl.pallas_call(functools.partial(grads_kernel, dims), out_shape=(sds((C,...]
    all_gather x10 -> x0, waiting for transfers between devices: 558 us -> none  [the longest x2 140 us: carried_in(): gathered = jax.tree.map(lambda a: lax.all_gather(a, axis), part)]
    psum x3 -> x0, waiting for transfers between devices: 142 us -> none  [the longest x1 50.4 us: shards(): grad_second = lax.psum(grad_second, 'tp')]
    all_gather x5 -> x0, blocking collectives: 82.5 us -> none  [the longest x1 20.2 us: shards(): lax.all_gather(norm1_bias, ('fsdp', 'ctx'), axis=0, tiled=True)]
    dot_general x36 -> x27, matrix products: 112 us -> 66.2 us  [the longest x15 59.2 us: dot(): return lax.dot_general(a, b, (dims, ((), ())), preferred_element_type=F32)]
    unnamed x1 -> x0, blocking collectives: 33.8 us -> none
  transfers between devices with their start and end apart: 21 -> 2, of which waited for: 21 -> 0; matrix products, arithmetic and copies ran while one was open for 6% -> 2% of each run, Pallas kernels for 0% -> 0%
where the time goes in v1:
time: 781 us; the launch traced here: 773 us
  Pallas kernels  596 us (76%)
  local copies, waits for them, and re-layouts  71 us (9%)
  matrix products  66.2 us (8%)
  other arithmetic  37.2 us (5%)
    pallas_call x1, Pallas kernels, shards(): pl.pallas_call(functools.partial(grads_kernel, dims), out_shape=(sds((C,...  189 us
    pallas_call x1, Pallas kernels, shards(): pl.pallas_call(functools.partial(first_kernel, dims), out_shape=(sds((F,...  154 us
    pallas_call x1, Pallas kernels, shards(): pl.pallas_call(functools.partial(mlp_kernel, dims), out_shape=(sds((Q, W)...  128 us
    pallas_call x1, Pallas kernels, shards(): pl.pallas_call(functools.partial(out_kernel, dims), out_shape=(sds((Q, W)...  76.1 us
    dot_general x15, matrix products, dot(): return lax.dot_general(a, b, (dims, ((), ())), preferred_element_type=F32)  59.2 us
    pallas_call x1, Pallas kernels, shards(): pl.pallas_call(functools.partial(last_kernel, dims), out_shape=(sds((T, Q...  49.2 us
    unnamed x130, local copies, waits for them, and re-layouts  22.9 us
  transfers between devices with their start and end apart: 2, of which 0 were waited for; matrix products, arithmetic and copies ran while one was open for 2% of the time, Pallas kernels for 0%

profile of v1, /device:TPU:14, one launch (start us, length us, event | category | flops | bytes accessed | tf_op | source)
XLA Modules:
  0.0 773.4 jit_solution(674431194104032794)
XLA Ops:
  0.7 2.0 fusion.83
  2.7 1.9 fusion.82
  5.6 1.0 fusion.84
  6.6 1.8 fusion.81
  11.4 1.6 maximum_bitcast_fusion
  13.0 1.6 pad_maximum_fusion.win
  14.6 1.3 maximum_bitcast_fusion.6
  16.1 1.6 pad_maximum_fusion.1.wrest
  18.4 153.7 %k_first.1 = (bf16[2,4,256,1024]{3,2,1,0:T(8,128)(2,1)}, bf16[2,4,256,1024]{3,2,1,0:T(8,128)(2,1)}, f32[2,4,8,256]{3,2,1,0:T(8,128)}, f32[4,8,256]{2,1,0:T(8,128...) custom-call(bf16[4,256,1024]{2,1,0:T(8,128)(2,1)} %pad_maximum_fusion.win, ...), custom_call_target="tpu_custom_call" | custom-call | tf_op jit(solution)/shard_map/k_first/pallas_call | solution.py:556
  172.8 1.2 reduce-window.6
  174.3 1.0 slice_bitcast_fusion
  175.9 2.8 convert_reduce_fusion
  178.8 1.2 multiply_reduce_fusion
  180.1 1.7 add_convert_fusion.1
  182.2 5.2 convolution_convert_fusion.7
  187.4 1.3 slice_convert_fusion
  189.1 1.5 fusion.13
  192.8 1.4 fusion.47
  196.5 4.7 fusion.37
  201.2 1.9 dynamic-slice_bitcast_fusion
  203.1 1.4 rsqrt.23
  206.9 4.7 convolution_convert_fusion.1
  211.6 76.1 %k_out.1 = (f32[64,2048]{1,0:T(8,128)}, bf16[4,4,64,2048]{3,2,1,0:T(8,128)(2,1)}) custom-call(bf16[4,4,64,2048]{3,2,1,0:T(8,128)(2,1)} %bitcast.214, bf16[64,2048]{1,0:T(8,128)(2,1)} %get-tuple-element.179.tok, f32[1,2048]{1,0:T(1,128)} %bitcast.270, f32[1,2048]{1,0:T(1,128)} %bitcast.275), custom_call_target="tpu_custom_call" | custom-call | tf_op jit(solution)/shard_map/k_out/pallas_call | solution.py:649
  287.7 3.9 convolution_convert_fusion.9
  291.8 4.2 fusion.21
  296.0 1.3 fusion.28
  297.3 3.6 convolution_convert_fusion
  301.0 3.6 add_convert_fusion
  304.6 128.2 %k_mlp.1 = (f32[64,2048]{1,0:T(8,128)}, bf16[4,4,64,2048]{3,2,1,0:T(8,128)(2,1)}, bf16[4,64,2048]{2,1,0:T(8,128)(2,1)}, f32[1,2048]{1,0:T(1,128)}, f32[1,2048]{1,0:T(1,128)}) custom-call(bf16[4,4,64,2048]{3,2,1,0:T(8,128)(2,1)} %bitcast.215, bf16[4,4,64,2048]{3,2,1,0:T(8,128)(2,1)} %bitcast.237, f32[64,2048]{1,0:T(8,128)} %get-tuple-element.39.mid, ...), custom_call_target="tpu_custom_call" | custom-call | tf_op jit(solution)/shard_map/k_mlp/pallas_call | solution.py:674
  432.8 5.4 multiply_reduce_fusion.2
  438.2 1.3 stack.106
  439.4 2.1 multiply_reduce_fusion.1
  442.1 1.3 pad_maximum_fusion.8
  443.4 4.6 fusion.3
  450.2 1.8 multiply_convert_fusion.1
  452.0 1.4 fusion.93
  455.2 1.4 fusion.49
  457.7 1.1 copy-done.51
  458.8 6.3 convolution_convert_fusion.2
  465.1 6.7 convert_dynamic-update-slice_fusion
  471.9 2.3 fusion.7
  474.4 2.3 fusion.6
  476.8 2.4 fusion.5
  479.2 2.5 fusion.4
  481.7 12.6 %copy.84 = bf16[2048,2048]{1,0:T(8,128)(2,1)} copy(bf16[2048,2048]{0,1:T(8,128)(2,1)} %fusion.4) | data formatting | bytes 16777216 | tf_op jit(solution)/shard_map/concatenate | solution.py:731
  494.3 49.2 %k_last.1 = (bf16[4,64,2048]{2,1,0:T(8,128)(2,1)}, f32[1,2048]{1,0:T(1,128)}, f32[1,2048]{1,0:T(1,128)}) custom-call(bf16[4,4,64,2048]{3,2,1,0:T(8,128)(2,1)} %bitcast.229, f32[64,2048]{1,0:T(8,128)} %get-tuple-element.42.gm, bf16[64,2048]{1,0:T(8,128)(2,1)} %get-tuple-element.179.tok, f32[1,2048]{1,0:T(1,128)} %bitcast.267), custom_call_target="tpu_custom_call" | custom-call | tf_op jit(solution)/shard_map/k_last/pallas_call | solution.py:718
  543.5 1.4 concatenate.56
  544.9 188.7 %k_grads.1 = (bf16[4,256,2048]{2,1,0:T(8,128)(2,1)}, f32[8,256]{1,0:T(8,128)}) custom-call(bf16[2,4,256,2048]{3,2,1,0:T(8,128)(2,1)} %bitcast.213, f32[2,4,8,256]{3,2,1,0:T(8,128)} %bitcast.263), custom_call_target="tpu_custom_call" | custom-call | tf_op jit(solution)/shard_map/k_grads/pallas_call | solution.py:744
  733.6 2.4 convert_reduce_fusion.1
  736.1 3.9 convert_bitcast_fusion
  739.9 2.0 copy.85
  742.0 2.0 copy.93
  744.0 2.0 copy.86
  746.0 2.0 copy.94
  748.1 2.5 copy.87
  750.6 2.5 copy.95
  753.1 2.5 copy.88
  755.7 2.5 copy.96
  758.2 2.5 copy.89
  760.7 2.5 copy.97
  763.9 1.3 copy.90
  765.2 2.5 copy.98
  768.0 1.3 copy.99
  769.7 1.3 copy.100
  (175 shorter events, 21.7 us)
Async XLA Ops:
  0.6 7.8 %copy-start.18 = (bf16[256,1024]{1,0:T(8,128)(2,1)S(1)}, bf16[256,1024]{1,0:T(8,128)(2,1)}, u32[]{:S(2)}) copy-start(bf16[256,1024]{1,0:T(8,128)(2,1)} %param.25) | copy-start | bytes 1572868
  0.7 8.5 %copy-start.19 = (bf16[256,1024]{1,0:T(8,128)(2,1)S(1)}, bf16[256,1024]{1,0:T(8,128)(2,1)}, u32[]{:S(2)}) copy-start(bf16[256,1024]{1,0:T(8,128)(2,1)} %param.24) | copy-start | bytes 1572868
  0.7 9.3 %copy-start.20 = (bf16[256,1024]{1,0:T(8,128)(2,1)S(1)}, bf16[256,1024]{1,0:T(8,128)(2,1)}, u32[]{:S(2)}) copy-start(bf16[256,1024]{1,0:T(8,128)(2,1)} %param.21) | copy-start | bytes 1572868
  0.7 10.1 %copy-start.54 = (bf16[256]{0:T(256)(128)(2,1)S(1)}, bf16[256]{0:T(256)(128)(2,1)}, u32[]{:S(2)}) copy-start(bf16[256]{0:T(256)(128)(2,1)} %param.28) | copy-start | bytes 1540
  0.7 10.0 %copy-start.55 = (bf16[256]{0:T(256)(128)(2,1)S(1)}, bf16[256]{0:T(256)(128)(2,1)}, u32[]{:S(2)}) copy-start(bf16[256]{0:T(256)(128)(2,1)} %param.27) | copy-start | bytes 1540
  0.7 10.1 %copy-start.56 = (bf16[256]{0:T(256)(128)(2,1)S(1)}, bf16[256]{0:T(256)(128)(2,1)}, u32[]{:S(2)}) copy-start(bf16[256]{0:T(256)(128)(2,1)} %param.23) | copy-start | bytes 1540
  0.7 10.1 %copy-start.57 = (bf16[256]{0:T(256)(128)(2,1)S(1)}, bf16[256]{0:T(256)(128)(2,1)}, u32[]{:S(2)}) copy-start(bf16[256]{0:T(256)(128)(2,1)} %param.22) | copy-start | bytes 1540
  0.7 10.1 %copy-start.48 = (f32[1,256,2]{1,2,0:T(2,128)S(1)}, f32[1,256,2]{1,2,0:T(2,128)}, u32[]{:S(2)}) copy-start(f32[1,256,2]{1,2,0:T(2,128)} %param.16) | copy-start | bytes 6148
  11.4 3.2 copy-start.22
  11.4 3.2 copy-start.23
  11.4 4.6 copy-start.21
  174.2 4.5 copy-start
  174.3 14.8 %copy-start.34 = (pred[256,256]{1,0:T(8,128)(4,1)}, pred[256,256]{1,0:T(8,128)(4,1)S(1)}, u32[]{:S(2)}) copy-start(pred[256,256]{1,0:T(8,128)(4,1)S(1)} %iota_compare_fusion) | copy-start | bytes 196612
  175.9 4.1 copy-start.29
  175.9 267.5 %copy-start.28 = (f32[1,2,4,256]{3,0,2,1:T(1,128)}, f32[1,2,4,256]{3,0,2,1:T(1,128)S(1)}, u32[]{:S(2)}) copy-start(f32[1,2,4,256]{3,0,2,1:T(1,128)S(1)} %get-tuple-element.151) | copy-start | bytes 24580
  180.0 1.8 copy-start.31
  180.1 2.2 copy-start.50
  188.7 5.4 copy-start.1
  188.7 5.5 copy-start.3
  189.1 3.7 copy-start.40
  189.1 3.7 copy-start.43
  189.1 5.1 copy-start.38
  189.1 5.1 copy-start.5
  190.7 4.1 copy-start.11
  194.2 0.7 copy-start.26
  194.7 1.8 copy-start.42
  195.3 0.6 copy-start.36
  196.5 8.6 %collective-permute-start = (f32[2,4,1,256]{3,1,2,0:T(4,128)}, f32[2,4,1,256]{3,1,2,0:T(4,128)}, u32[]{:S(2)}, u32[]{:S(2)}) collective-permute-start(f32[2,4,1,256]{3,1,2,0:T(4,128)} %pad_maximum_fusion.7), channel_id=1, source_target_pairs={{0,4},{4,0},{8,12},{12,8},{1,5},{5,1},{9,13},{13,9},{2,6},{6,2},{1... | collective-permute-start | bytes 24584 | tf_op jit(solution)/shard_map/ppermute | solution.py:632
  205.8 0.6 copy-start.32
  205.8 1.0 copy-start.33
  206.9 4.7 copy-start.8
  287.7 3.9 copy-start.10
  287.7 4.1 copy-start.14
  291.8 5.6 copy-start.58
  296.0 1.3 copy-start.16
  296.0 5.0 copy-start.24
  432.8 10.6 %copy-start.30 = (f32[1,2,4,256]{3,0,2,1:T(1,128)S(1)}, f32[1,2,4,256]{3,0,2,1:T(1,128)}, u32[]{:S(2)}) copy-start(f32[1,2,4,256]{3,0,2,1:T(1,128)} %copy-done.29) | copy-start | bytes 24580
  441.5 0.6 copy-start.37
  443.4 6.0 collective-permute-start.1
  448.0 5.5 copy-start.39
  448.0 6.0 copy-start.44
  449.4 4.1 copy-start.6
  449.4 4.7 copy-start.2
  449.4 4.7 copy-start.35
  452.0 2.9 copy-start.4
  454.1 2.5 copy-start.27
  454.1 2.5 copy-start.41
  456.6 2.2 copy-start.51
  458.8 6.3 copy-start.7
  465.1 6.7 copy-start.9
  465.1 6.7 copy-start.53
  471.9 2.3 copy-start.17
  471.9 2.6 copy-start.52
  474.4 2.3 copy-start.15
  474.4 2.3 copy-start.25
  476.8 2.4 copy-start.49
  476.8 2.4 copy-start.59
  494.3 49.2 %copy-start.45 = (f32[1,2048]{1,0:T(1,128)S(1)}, f32[1,2048]{1,0:T(1,128)}, u32[]{:S(2)}) copy-start(f32[1,2048]{1,0:T(1,128)} %get-tuple-element.46) | copy-start | bytes 24580
  494.3 49.2 %copy-start.46 = (f32[1,2048]{1,0:T(1,128)S(1)}, f32[1,2048]{1,0:T(1,128)}, u32[]{:S(2)}) copy-start(f32[1,2048]{1,0:T(1,128)} %get-tuple-element.47) | copy-start | bytes 24580
  753.1 10.1 %copy-start.47 = (f32[8,256]{1,0:T(8,128)S(1)}, f32[8,256]{1,0:T(8,128)}, u32[]{:S(2)}) copy-start(f32[8,256]{1,0:T(8,128)} %get-tuple-element.49) | copy-start | bytes 24580
  769.3 1.7 copy-start.12
  769.7 2.3 copy-start.13
